TPU v7x, 32 devices: a whole 2x2x4 slice. The times are simulated.
32 devices in a mesh: mem: 8 (over z, x), geo: 4 (over y, core).
Axes of the slice: x: 2, y: 2, z: 4, core: 2. Of those that a mesh axis runs over, the one named last changes fastest.
Arguments:
- control: float32 [8, 32, 48, 384], P('mem', 'geo'), may hold values from -6 to 6
- kappa_table: float32 [16], replicated, may hold values from 0.02 to 0.24
- kappa_index: int32 [48, 384], replicated, may hold values from 0 to 15
- tile_bounds: int32 [5], replicated, may hold values from 0 to 18432, as said below
- filter_bands: float32 [4, 5, 32], replicated, may hold values from -0.3 to 0.3
- perturbation: bfloat16 [2, 8, 32, 18432], P(None, 'mem', None, 'geo'), may hold values from -6 to 6
Outputs:
- increment: float32 [2, 32, 18432], P(None, 'mem', 'geo')
Inputs may be any that keep to these rules, and one draw needn't show every extreme that they name: tile_bounds[0] is 0, tile_bounds[4] is 18432, and the bounds never fall; tile t holds columns tile_bounds[t] to tile_bounds[t + 1] - 1.
All inputs are finite; a program needn't handle non-finite values.
Results may differ from a plain program's by a relative error of at most 0.005.
Values may be sent and summed in bfloat16 or wider, within the bound.
A program may use at most 64 MiB of HBM per device.

v0:
```python
import jax
import jax.numpy as jnp
from jax import lax
from jax.sharding import PartitionSpec as P

ITERS = 10


def neighbours(state):
    east = jnp.concatenate([state[..., 1:, :], state[..., -1:, :]], axis=-2)
    west = jnp.concatenate([state[..., :1, :], state[..., :-1, :]], axis=-2)
    north = jnp.concatenate([state[..., 1:], state[..., -1:]], axis=-1)
    south = jnp.concatenate([state[..., :1], state[..., :-1]], axis=-1)
    return (east, west, north, south)


def face_weights(kappa_field):
    return tuple((0.5 * (kappa_field + other) for other in neighbours(kappa_field)))


def diffuse_step(state, weights):
    east, west, north, south = neighbours(state)
    update = weights[0] * (east - state) + weights[1] * (west - state)
    update = update + weights[2] * (north - state) + weights[3] * (south - state)
    return state + update


def vertical_filter(values, coefficients):
    levels = values.shape[0]
    padded = jnp.pad(values, ((2, 2), (0, 0)))
    result = values
    for offset in range(5):
        result = result + coefficients[offset] * padded[offset : offset + levels]
    return result


def body(control, kappa_table, kappa_index, tile_bounds, filter_bands, perturbation):
    moved_pert = lax.all_to_all(perturbation, "mem", split_axis=2, concat_axis=1, tiled=True)
    kappa_field = jnp.zeros(kappa_index.shape, jnp.float32)
    for entry in range(kappa_table.shape[0]):
        kappa_field = kappa_field + jnp.where(kappa_index == entry, kappa_table[entry], 0.0)
    weights = face_weights(kappa_field)
    state_field = lax.fori_loop(0, ITERS, lambda step, cur: diffuse_step(cur, weights), control)
    flattened = state_field.reshape(state_field.shape[0], state_field.shape[1], -1)
    by_columns = lax.all_to_all(flattened, "geo", split_axis=2, concat_axis=1, tiled=True)
    width = by_columns.shape[2]
    tiles_count = filter_bands.shape[0]
    columns = lax.axis_index("geo") * width + jnp.arange(width, dtype=jnp.int32)
    tile_ids = jnp.sum((columns[None, :] >= tile_bounds[1:-1][:, None]).astype(jnp.int32), axis=0)
    one_hot = (tile_ids[None, :] == jnp.arange(tiles_count, dtype=jnp.int32)[:, None]).astype(
        jnp.float32
    )
    coefficients = jnp.einsum("tkl,tc->klc", filter_bands, one_hot, precision=lax.Precision.HIGHEST)
    filtered = vertical_filter(by_columns[0], coefficients).astype(jnp.bfloat16)
    moved_filtered = lax.all_to_all(filtered[None], "mem", split_axis=1, concat_axis=0, tiled=True)
    return jnp.sum(
        moved_pert.astype(jnp.float32) * moved_filtered.astype(jnp.float32)[None], axis=1
    )


def solution(mesh):
    in_specs = (P("mem", "geo", None, None), P(), P(), P(), P(), P(None, "mem", None, "geo"))
    out_specs = P(None, "mem", "geo")
    return jax.shard_map(body, mesh=mesh, in_specs=in_specs, out_specs=out_specs, check_vma=False)
```

profile of v0, /device:TPU:0, one launch (start us, length us, event | category | flops | bytes accessed | tf_op | source)
XLA Modules:
  0.0 219.2 jit_solution(1623861114880907975)
XLA Ops:
  0.0 1.1 copy.36
  1.1 1.9 fusion.36
  3.0 10.8 %select_add_fusion = f32[48,384]{1,0:T(8,128)S(1)} fusion(s32[48,384]{1,0:T(8,128)} %param.10, f32[]{:T(128)} %bitcast.16, f32[]{:T(128)} %bitcast.15, f32[]{:T(128)} %bitcast.14, f32[]{:T(128)} %bitcast.13, f32[]{:T(128)} %bitcast.12, f32[]{:T(128)} %bitcast.11, f32[]{:T(128)} %bitcast.10, f32[]{:T(128)} %bitcast.9, f32[]{:T(128)} %bitcast.8, f32[]{:T(128)} %bitcast.7, ...), kind=kLoop, calls=%fused_computation.47 | loop fusion | flops 866304 | bytes 147520 | tf_op jit(solution)/shard_map/add | solution.py:41
  14.1 10.9 %fusion.24 = (f32[48,384]{1,0:T(8,128)S(1)}, f32[48,384]{1,0:T(8,128)S(1)}, f32[48,384]{1,0:T(8,128)S(1)}, f32[48,384]{1,0:T(8,128)S(1)}) fusion(f32[48,383]{1,0:T(8,128)S(1)} %get-tuple-element.64, f32[48,1]{1,0:T(8,128)S(1)} %get-tuple-element.62, f32[48,1]{1,0:T(8,128)S(1)} %get-tuple-element.63, f32[48,383]{1,0:T(8,128)S(1)} %get-tuple-element.65, ...), kind=kLoop, calls=%fused_computation.44 | loop fusion | flops 1087488 | bytes 663616 | tf_op jit(solution)/shard_map/mul | solution.py:18
  24.9 10.2 %while.10 = (s32[]{:T(128)}, f32[1,8,48,384]{3,2,1,0:T(8,128)S(1)}, f32[48,384]{1,0:T(8,128)S(1)}, f32[48,384]{1,0:T(8,128)S(1)}, f32[48,384]{1,0:T(8,128)S(1)}, /*index=5*/f32[48,384]{1,0:T(8,128)S(1)}, s32[]{:T(128)}) while((s32[]{:T(128)}, f32[1,8,48,384]{3,2,1,0:T(8,128)S(1)}, f32[48,384]{1,0:T(8,128)S(1)}, f32[48,384]{1,0:T(8,128)S(1)}, ...), condition=%wide.region_1.2_spmd, body=%wide.region_0.1_spmd.sunk | while | flops 2359298 | bytes 8552525 | solution.py:43
  25.0 0.2 fusion.46
  25.4 0.6 fusion.47
  26.1 0.2 fusion.46
  26.4 0.6 fusion.47
  27.1 0.2 fusion.46
  27.4 0.6 fusion.47
  28.1 0.2 fusion.46
  28.5 0.6 fusion.47
  29.1 0.2 fusion.46
  29.5 0.6 fusion.47
  30.1 0.2 fusion.46
  30.5 0.6 fusion.47
  31.2 0.2 fusion.46
  31.5 0.6 fusion.47
  32.2 0.2 fusion.46
  32.5 0.6 fusion.47
  33.2 0.2 fusion.46
  33.6 0.6 fusion.47
  34.6 0.6 fusion.47
  35.2 5.5 %copy.21 = f32[1,8,48,384]{1,3,2,0:T(8,128)} copy(f32[1,8,48,384]{3,2,1,0:T(8,128)S(1)} %get-tuple-element.37) | data formatting | bytes 1179648 | tf_op jit(solution)/shard_map/while | solution.py:43
  40.7 0.5 broadcast.28
  41.2 83.6 %reduce.2 = f32[18432,8]{1,0:T(8,128)} reduce(f32[18432,1,8]{2,1,0:T(1,128)} %bitcast.70, f32[]{:T(128)} %broadcast.28), dimensions={1}, to_apply=%bitcast.62.reduce_sub_computation | reduce | bytes 1179652
  124.8 7.8 %reshape.43 = f32[4,1,36864]{2,1,0:T(1,128)} reshape(f32[18432,8]{1,0:T(8,128)} %reduce.2) | data formatting | bytes 1179648
  132.6 4.3 %all-to-all-start.1 = ((f32[4,1,36864]{2,1,0:T(1,128)}), f32[4,1,36864]{2,1,0:T(1,128)}, u32[]{:S(2)}, u32[]{:S(2)}) async-start(f32[4,1,36864]{2,1,0:T(1,128)} %reshape.43), calls=%async_computation.1 | async-start | bytes 1179648 | tf_op jit(solution)/shard_map/all_to_all | solution.py:45
  137.2 1.3 convolution_bitcast_fusion
  138.5 8.5 %all-to-all-done.1 = f32[4,1,36864]{2,1,0:T(1,128)} async-done(((f32[4,1,36864]{2,1,0:T(1,128)}), f32[4,1,36864]{2,1,0:T(1,128)}, u32[]{:S(2)}, u32[]{:S(2)}) %all-to-all-start.1) | async-done | bytes 589856 | tf_op jit(solution)/shard_map/all_to_all | solution.py:45
  147.0 3.3 %reduce.3 = f32[4,36864]{1,0:T(4,128)S(1)} reduce(f32[4,1,36864]{2,1,0:T(1,128)} %all-to-all-done.1, f32[]{:T(128)} %broadcast.28), dimensions={1}, to_apply=%all_to_all.11.reduce_sub_computation | reduce | bytes 1179652 | tf_op jit(solution)/shard_map/all_to_all | solution.py:45
  150.3 22.3 %reshape.44 = f32[18432,1,8]{2,1,0:T(1,128)} reshape(f32[4,36864]{1,0:T(4,128)S(1)} %reduce.3) | data formatting | bytes 1179648
  172.6 5.5 %copy.22 = f32[1,8,4,4608]{3,1,2,0:T(8,128)S(1)} copy(f32[1,8,4,4608]{1,3,2,0:T(8,128)} %bitcast.71) | data formatting | bytes 1179648 | tf_op jit(solution)/shard_map/all_to_all | solution.py:45
  178.1 0.4 fusion.20
  178.5 0.5 copy.27
  178.9 0.5 broadcast.30
  179.5 2.5 %reduce.4 = bf16[32,4608]{1,0:T(8,128)(2,1)S(1)} reduce(bf16[32,1,4608]{2,1,0:T(2,128)(2,1)S(1)} %bitcast.72, bf16[]{:T(256)} %broadcast.30), dimensions={1}, to_apply=%bitcast.69.reduce_sub_computation | reduce | bytes 589826
  181.9 0.9 reshape.45
  182.8 6.6 %all-to-all-start.2 = ((bf16[8,2,9216]{2,1,0:T(2,128)(2,1)}), bf16[8,2,9216]{2,1,0:T(2,128)(2,1)S(1)}, u32[]{:S(2)}, u32[]{:S(2)}) async-start(bf16[8,2,9216]{2,1,0:T(2,128)(2,1)} %reshape.45), calls=%async_computation.2 | async-start | bytes 589824 | tf_op jit(solution)/shard_map/all_to_all | solution.py:55
  189.4 1.4 copy.20
  190.8 7.9 %all-to-all-done.2 = bf16[8,2,9216]{2,1,0:T(2,128)(2,1)S(1)} async-done(((bf16[8,2,9216]{2,1,0:T(2,128)(2,1)}), bf16[8,2,9216]{2,1,0:T(2,128)(2,1)S(1)}, u32[]{:S(2)}, u32[]{:S(2)}) %all-to-all-start.2) | async-done | bytes 294944 | tf_op jit(solution)/shard_map/all_to_all | solution.py:55
  198.7 3.6 %all-to-all-start = ((bf16[2,1,32,4608]{3,0,1,2:T(2,128)(2,1)}), bf16[2,1,32,4608]{3,0,1,2:T(2,128)(2,1)S(1)}, u32[]{:S(2)}, u32[]{:S(2)}) async-start(bf16[2,1,32,4608]{3,0,1,2:T(2,128)(2,1)} %copy.20), calls=%async_computation | async-start | bytes 1179648 | tf_op jit(solution)/shard_map/all_to_all | solution.py:38
  202.3 0.2 reshape.46
  202.6 1.7 convert_reduce_fusion
  204.5 13.4 %all-to-all-done = bf16[2,1,32,4608]{3,0,1,2:T(2,128)(2,1)S(1)} async-done(((bf16[2,1,32,4608]{3,0,1,2:T(2,128)(2,1)}), bf16[2,1,32,4608]{3,0,1,2:T(2,128)(2,1)S(1)}, u32[]{:S(2)}, u32[]{:S(2)}) %all-to-all-start) | async-done | bytes 589856 | tf_op jit(solution)/shard_map/all_to_all | solution.py:38
  217.9 0.6 fusion.8
  218.5 0.7 copy.24
  (45 shorter events, 2.9 us)
Async XLA Ops:
  0.0 137.2 %copy-start = (f32[4,5,32]{2,0,1:T(4,128)S(1)}, f32[4,5,32]{2,0,1:T(4,128)}, u32[]{:S(2)}) copy-start(f32[4,5,32]{2,0,1:T(4,128)} %param.12) | copy-start | bytes 7684
  124.8 12.2 %copy-start.2 = (s32[5]{0:T(128)S(1)}, s32[5]{0:T(128)}, u32[]{:S(2)}) copy-start(s32[5]{0:T(128)} %param.11) | copy-start | bytes 64
  132.6 14.4 %all-to-all-start.1 = ((f32[4,1,36864]{2,1,0:T(1,128)}), f32[4,1,36864]{2,1,0:T(1,128)}, u32[]{:S(2)}, u32[]{:S(2)}) async-start(f32[4,1,36864]{2,1,0:T(1,128)} %reshape.43), calls=%async_computation.1 | async-start | bytes 1179648 | tf_op jit(solution)/shard_map/all_to_all | solution.py:45
  178.5 10.9 %copy-start.1 = (bf16[2,1,32,4608]{3,2,1,0:T(8,128)(2,1)S(1)}, bf16[2,1,32,4608]{3,2,1,0:T(8,128)(2,1)}, u32[]{:S(2)}) copy-start(bf16[2,1,32,4608]{3,2,1,0:T(8,128)(2,1)} %param.13) | copy-start | bytes 1769476
  182.8 15.8 %all-to-all-start.2 = ((bf16[8,2,9216]{2,1,0:T(2,128)(2,1)}), bf16[8,2,9216]{2,1,0:T(2,128)(2,1)S(1)}, u32[]{:S(2)}, u32[]{:S(2)}) async-start(bf16[8,2,9216]{2,1,0:T(2,128)(2,1)} %reshape.45), calls=%async_computation.2 | async-start | bytes 589824 | tf_op jit(solution)/shard_map/all_to_all | solution.py:55
  198.7 19.2 %all-to-all-start = ((bf16[2,1,32,4608]{3,0,1,2:T(2,128)(2,1)}), bf16[2,1,32,4608]{3,0,1,2:T(2,128)(2,1)S(1)}, u32[]{:S(2)}, u32[]{:S(2)}) async-start(bf16[2,1,32,4608]{3,0,1,2:T(2,128)(2,1)} %copy.20), calls=%async_computation | async-start | bytes 1179648 | tf_op jit(solution)/shard_map/all_to_all | solution.py:38
where the time goes:
time: 220 us; the launch traced here: 219 us
  other arithmetic  119 us (54%)
  local copies, waits for them, and re-layouts  53.6 us (24%)
  waiting for transfers between devices  29.8 us (14%)
  starting transfers between devices  14.5 us (7%)
    unnamed x2, other arithmetic  86 us
    unnamed x14, local copies, waits for them, and re-layouts  34.8 us
    all_to_all x1, waiting for transfers between devices, body(): lax.all_to_all(perturbation, 'mem', split_axis=2, concat_axis=1, tiled=True)  13.4 us
    mul x1, other arithmetic, face_weights(): 0.5 * (kappa_field + other)  10.9 us
    add x1, other arithmetic, body(): kappa_field + jnp.where(kappa_index == entry, kappa_table[entry], 0.0)  10.8 us
    all_to_all x1, waiting for transfers between devices, body(): lax.all_to_all(flattened, 'geo', split_axis=2, concat_axis=1, tiled=True)  8.52 us
    all_to_all x1, waiting for transfers between devices, body(): lax.all_to_all(filtered[None], 'mem', split_axis=1, concat_axis=0, tiled=...  7.85 us
    all_to_all x1, starting transfers between devices, body(): lax.all_to_all(filtered[None], 'mem', split_axis=1, concat_axis=0, tiled=...  6.57 us
  transfers between devices with their start and end apart: 3, of which 3 were waited for; matrix products, arithmetic and copies ran while one was open for 2% of the time, Pallas kernels for 0%

commit v1 on v0

--- a/solution.py
+++ b/solution.py
@@ -4,6 +4,22 @@
 from jax.sharding import PartitionSpec as P
 
 ITERS = 10
+
+
+def swapped_with_each(x, axis, split, join):
+    ways, here = (lax.axis_size(axis), lax.axis_index(axis))
+    width = x.shape[split] // ways
+    shape = list(x.shape)
+    shape[split] = width
+    height = shape[join]
+    shape[join] = height * ways
+    full = jnp.zeros(shape, x.dtype)
+    for mask in range(ways):
+        part = lax.dynamic_slice_in_dim(x, (here ^ mask) * width, width, axis=split)
+        if mask:
+            part = lax.ppermute(part, axis, [(d, d ^ mask) for d in range(ways)])
+        full = lax.dynamic_update_slice_in_dim(full, part, (here ^ mask) * height, axis=join)
+    return full
 
 
 def neighbours(state):
@@ -42,7 +58,7 @@
     weights = face_weights(kappa_field)
     state_field = lax.fori_loop(0, ITERS, lambda step, cur: diffuse_step(cur, weights), control)
     flattened = state_field.reshape(state_field.shape[0], state_field.shape[1], -1)
-    by_columns = lax.all_to_all(flattened, "geo", split_axis=2, concat_axis=1, tiled=True)
+    by_columns = swapped_with_each(flattened, "geo", 2, 1)
     width = by_columns.shape[2]
     tiles_count = filter_bands.shape[0]
     columns = lax.axis_index("geo") * width + jnp.arange(width, dtype=jnp.int32)

time: 220 us -> 90.3 us (0.41)
  other arithmetic: 119 us -> 32.8 us
  local copies, waits for them, and re-layouts: 53.6 us -> 15.7 us
  waiting for transfers between devices: 29.8 us -> 26.6 us
    unnamed x2 -> x1, other arithmetic: 86 us -> 2.45 us
    unnamed x14 -> x11, local copies, waits for them, and re-layouts: 34.8 us -> 4.17 us
    all_to_all x1 -> x0, waiting for transfers between devices: 8.52 us -> none  [body(): lax.all_to_all(flattened, 'geo', split_axis=2, concat_axis=1, tiled=True)]
    while x1 -> x0, local copies, waits for them, and re-layouts: 5.53 us -> none  [body(): lax.fori_loop(0, ITERS, lambda step, cur: diffuse_step(cur, weights), con...]
    all_to_all x1 -> x0, local copies, waits for them, and re-layouts: 5.48 us -> none  [body(): lax.all_to_all(flattened, 'geo', split_axis=2, concat_axis=1, tiled=True)]
    all_to_all x1 -> x0, starting transfers between devices: 4.32 us -> none  [body(): lax.all_to_all(flattened, 'geo', split_axis=2, concat_axis=1, tiled=True)]
    ppermute x0 -> x3, waiting for transfers between devices: none -> 4.16 us  [swapped_with_each(): part = lax.ppermute(part, axis, [(d, d ^ mask) for d in range(ways)])]
    all_to_all x1 -> x0, other arithmetic: 3.25 us -> none  [body(): lax.all_to_all(flattened, 'geo', split_axis=2, concat_axis=1, tiled=True)]
  transfers between devices with their start and end apart: 3 -> 5, of which waited for: 3 -> 4; matrix products, arithmetic and copies ran while one was open for 2% -> 8% of each run, Pallas kernels for 0% -> 0%
where the time goes in v1:
time: 90.3 us; the launch traced here: 89.5 us
  other arithmetic  32.8 us (36%)
  waiting for transfers between devices  26.6 us (29%)
  local copies, waits for them, and re-layouts  15.7 us (17%)
  starting transfers between devices  12.5 us (14%)
  matrix products  1.34 us (1%)
    all_to_all x1, waiting for transfers between devices, body(): lax.all_to_all(perturbation, 'mem', split_axis=2, concat_axis=1, tiled=True)  13.9 us
    mul x1, other arithmetic, face_weights(): 0.5 * (kappa_field + other)  11 us
    add x1, other arithmetic, body(): kappa_field + jnp.where(kappa_index == entry, kappa_table[entry], 0.0)  11 us
    all_to_all x1, waiting for transfers between devices, body(): lax.all_to_all(filtered[None], 'mem', split_axis=1, concat_axis=0, tiled=...  8.6 us
    all_to_all x1, starting transfers between devices, body(): lax.all_to_all(filtered[None], 'mem', split_axis=1, concat_axis=0, tiled=...  5.75 us
    add x10, other arithmetic, diffuse_step(): return state + update  5.46 us
    unnamed x11, local copies, waits for them, and re-layouts  4.17 us
    ppermute x3, waiting for transfers between devices, swapped_with_each(): part = lax.ppermute(part, axis, [(d, d ^ mask) for d in range(ways)])  4.16 us
  transfers between devices with their start and end apart: 5, of which 4 were waited for; matrix products, arithmetic and copies ran while one was open for 8% of the time, Pallas kernels for 0%

profile of v1, /device:TPU:0, one launch (start us, length us, event | category | flops | bytes accessed | tf_op | source)
XLA Modules:
  0.0 89.5 jit_solution(14284369988036795165)
XLA Ops:
  0.0 1.1 %copy.31 = f32[1,8,48,384]{3,2,1,0:T(8,128)S(1)} copy(f32[1,8,48,384]{3,2,1,0:T(8,128)} %param.8) | data formatting | bytes 1179648
  1.1 2.0 %fusion.36 = (f32[1]{0:T(128)}, f32[1]{0:T(128)}, f32[1]{0:T(128)}, f32[1]{0:T(128)}, f32[1]{0:T(128)}, /*index=5*/f32[1]{0:T(128)}, f32[1]{0:T(128)}, f32[1]{0:...) fusion(f32[16]{0:T(128)} %param.9), kind=kLoop, calls=%fused_computation.66 | loop fusion | bytes 128 | tf_op jit(solution)/shard_map/slice | solution.py:57
  3.0 11.0 %select_add_fusion = f32[48,384]{1,0:T(8,128)S(1)} fusion(s32[48,384]{1,0:T(8,128)} %param.10, f32[]{:T(128)} %bitcast.16, f32[]{:T(128)} %bitcast.15, f32[]{:T(128)} %bitcast.14, f32[]{:T(128)} %bitcast.13, f32[]{:T(128)} %bitcast.12, f32[]{:T(128)} %bitcast.11, f32[]{:T(128)} %bitcast.10, f32[]{:T(128)} %bitcast.9, f32[]{:T(128)} %bitcast.8, f32[]{:T(128)} %bitcast.7, ...), kind=kLoop, calls=%fused_computation.51 | loop fusion | flops 866304 | bytes 147520 | tf_op jit(solution)/shard_map/add | solution.py:57
  14.2 11.0 %fusion.24 = (f32[48,384]{1,0:T(8,128)S(1)}, f32[48,384]{1,0:T(8,128)S(1)}, f32[48,384]{1,0:T(8,128)S(1)}, f32[48,384]{1,0:T(8,128)S(1)}) fusion(f32[48,383]{1,0:T(8,128)S(1)} %get-tuple-element.67, f32[48,1]{1,0:T(8,128)S(1)} %get-tuple-element.65, f32[48,1]{1,0:T(8,128)S(1)} %get-tuple-element.66, f32[48,383]{1,0:T(8,128)S(1)} %get-tuple-element.68, ...), kind=kLoop, calls=%fused_computation.48 | loop fusion | flops 1087488 | bytes 663616 | tf_op jit(solution)/shard_map/mul | solution.py:34
  25.3 10.2 %while.10 = (s32[]{:T(128)}, f32[1,8,48,384]{3,2,1,0:T(8,128)S(1)}, f32[48,384]{1,0:T(8,128)S(1)}, f32[48,384]{1,0:T(8,128)S(1)}, f32[48,384]{1,0:T(8,128)S(1)}, /*index=5*/f32[48,384]{1,0:T(8,128)S(1)}, s32[]{:T(128)}) while((s32[]{:T(128)}, f32[1,8,48,384]{3,2,1,0:T(8,128)S(1)}, f32[48,384]{1,0:T(8,128)S(1)}, f32[48,384]{1,0:T(8,128)S(1)}, ...), condition=%wide.region_1.2_spmd, body=%wide.region_0.1_spmd.sunk | while | flops 2359298 | bytes 8552525 | solution.py:59
  25.4 0.2 fusion.46
  25.7 0.5 fusion.47
  26.4 0.2 fusion.46
  26.8 0.5 fusion.47
  27.4 0.2 fusion.46
  27.8 0.5 fusion.47
  28.4 0.2 fusion.46
  28.8 0.5 fusion.47
  29.4 0.2 fusion.46
  29.8 0.5 fusion.47
  30.5 0.2 fusion.46
  30.8 0.5 fusion.47
  31.5 0.2 fusion.46
  31.8 0.5 fusion.47
  32.5 0.2 fusion.46
  32.9 0.5 fusion.47
  33.5 0.2 fusion.46
  33.9 0.5 fusion.47
  34.5 0.2 fusion.46
  34.9 0.5 fusion.47
  35.6 0.8 constant_dynamic-slice_fusion
  36.3 0.5 collective-permute-start
  36.8 2.5 %collective-permute-start.1 = (f32[1,8,4608]{2,1,0:T(8,128)}, f32[1,8,4608]{2,1,0:T(8,128)}, u32[]{:S(2)}, u32[]{:S(2)}) collective-permute-start(f32[1,8,4608]{2,1,0:T(8,128)} %get-tuple-element.59), channel_id=1, source_target_pairs={{0,2},{1,3},{2,0},{3,1},{4,6},{5,7},{6,4},{7,5},{8,10},{9,11},{10,... | collective-permute-start | bytes 442376 | tf_op jit(solution)/shard_map/ppermute | solution.py:20
  39.8 1.3 %convolution_bitcast_fusion = f32[5,32,4608]{2,1,0:T(8,128)S(1)} fusion(f32[4,5,32]{2,0,1:T(4,128)S(1)} %copy-done, s32[4608]{0:T(1024)S(1)} %convert_reduce_fusion.1), kind=kOutput, calls=%fused_computation.12 | convolution fusion | flops 35407872 | bytes 2970112 | tf_op jit(solution)/shard_map/tkl,tc->klc/dot_general | solution.py:69
  41.1 0.9 %bitcast_dynamic-update-slice_fusion.2 = f32[32,4608]{1,0:T(8,128)S(1)} fusion(f32[32,4608]{1,0:T(8,128)S(1)} %bitcast_dynamic-update-slice_fusion.3, s32[]{:T(128)S(6)} %select_n.92, f32[1,8,4608]{2,1,0:T(8,128)} %collective-permute-done), kind=kLoop, calls=%fused_computation.39 | loop fusion | bytes 294916 | tf_op jit(solution)/shard_map/dynamic_update_slice | solution.py:21
  42.1 2.3 %collective-permute-done.1 = f32[1,8,4608]{2,1,0:T(8,128)} collective-permute-done((f32[1,8,4608]{2,1,0:T(8,128)}, f32[1,8,4608]{2,1,0:T(8,128)}, u32[]{:S(2)}, u32[]{:S(2)}) %collective-permute-start.1) | collective-permute-done | bytes 147488 | tf_op jit(solution)/shard_map/ppermute | solution.py:20
  44.4 0.9 %bitcast_dynamic-update-slice_fusion.1 = f32[32,4608]{1,0:T(8,128)S(1)} fusion(f32[32,4608]{1,0:T(8,128)S(1)} %bitcast_dynamic-update-slice_fusion.2, s32[]{:T(128)S(6)} %select_n.94, f32[1,8,4608]{2,1,0:T(8,128)} %collective-permute-done.1), kind=kLoop, calls=%fused_computation.38 | loop fusion | bytes 294916 | tf_op jit(solution)/shard_map/dynamic_update_slice | solution.py:21
  45.3 1.9 %collective-permute-done.2 = f32[1,8,4608]{2,1,0:T(8,128)} collective-permute-done((f32[1,8,4608]{2,1,0:T(8,128)}, f32[1,8,4608]{2,1,0:T(8,128)}, u32[]{:S(2)}, u32[]{:S(2)}) %collective-permute-start.2) | collective-permute-done | bytes 147488 | tf_op jit(solution)/shard_map/ppermute | solution.py:20
  47.2 0.9 %bitcast_dynamic-update-slice_fusion = f32[32,4608]{1,0:T(8,128)S(1)} fusion(f32[32,4608]{1,0:T(8,128)S(1)} %bitcast_dynamic-update-slice_fusion.1, s32[]{:T(128)S(6)} %select_n.96, f32[1,8,4608]{2,1,0:T(8,128)} %collective-permute-done.2), kind=kLoop, calls=%fused_computation.37 | loop fusion | bytes 294916 | tf_op jit(solution)/shard_map/dynamic_update_slice | solution.py:21
  48.1 0.4 fusion.20
  48.5 0.5 copy.19
  48.9 0.5 broadcast.30
  49.4 2.4 %reduce.2 = bf16[32,4608]{1,0:T(8,128)(2,1)S(1)} reduce(bf16[32,1,4608]{2,1,0:T(2,128)(2,1)S(1)} %bitcast.73, bf16[]{:T(256)} %broadcast.30), dimensions={1}, to_apply=%bitcast.72.reduce_sub_computation | reduce | bytes 589826
  51.9 0.9 %reshape.50 = bf16[8,2,9216]{2,1,0:T(2,128)(2,1)} reshape(bf16[32,4608]{1,0:T(8,128)(2,1)S(1)} %reduce.2) | data formatting | bytes 589824
  52.8 5.7 %all-to-all-start.1 = ((bf16[8,2,9216]{2,1,0:T(2,128)(2,1)}), bf16[8,2,9216]{2,1,0:T(2,128)(2,1)S(1)}, u32[]{:S(2)}, u32[]{:S(2)}) async-start(bf16[8,2,9216]{2,1,0:T(2,128)(2,1)} %reshape.50), calls=%async_computation.1 | async-start | bytes 589824 | tf_op jit(solution)/shard_map/all_to_all | solution.py:71
  58.5 1.4 %copy.14 = bf16[2,1,32,4608]{3,0,1,2:T(2,128)(2,1)} copy(bf16[2,1,32,4608]{3,2,1,0:T(8,128)(2,1)S(1)} %copy-done.1) | data formatting | bytes 1179648 | tf_op args[5]
  60.0 8.6 %all-to-all-done.1 = bf16[8,2,9216]{2,1,0:T(2,128)(2,1)S(1)} async-done(((bf16[8,2,9216]{2,1,0:T(2,128)(2,1)}), bf16[8,2,9216]{2,1,0:T(2,128)(2,1)S(1)}, u32[]{:S(2)}, u32[]{:S(2)}) %all-to-all-start.1) | async-done | bytes 294944 | tf_op jit(solution)/shard_map/all_to_all | solution.py:71
  68.6 3.6 %all-to-all-start = ((bf16[2,1,32,4608]{3,0,1,2:T(2,128)(2,1)}), bf16[2,1,32,4608]{3,0,1,2:T(2,128)(2,1)S(1)}, u32[]{:S(2)}, u32[]{:S(2)}) async-start(bf16[2,1,32,4608]{3,0,1,2:T(2,128)(2,1)} %copy.14), calls=%async_computation | async-start | bytes 1179648 | tf_op jit(solution)/shard_map/all_to_all | solution.py:54
  72.2 0.2 reshape.51
  72.5 1.7 %convert_reduce_fusion = f32[32,4608]{1,0:T(8,128)S(1)} fusion(bf16[32,1,4608]{2,1,0:T(2,128)(2,1)S(1)} %reshape.51), kind=kLoop, calls=%fused_computation.35 | loop fusion | flops 147456 | bytes 884736 | tf_op jit(solution)/shard_map/convert_element_type | solution.py:73
  74.3 13.9 %all-to-all-done = bf16[2,1,32,4608]{3,0,1,2:T(2,128)(2,1)S(1)} async-done(((bf16[2,1,32,4608]{3,0,1,2:T(2,128)(2,1)}), bf16[2,1,32,4608]{3,0,1,2:T(2,128)(2,1)S(1)}, u32[]{:S(2)}, u32[]{:S(2)}) %all-to-all-start) | async-done | bytes 589856 | tf_op jit(solution)/shard_map/all_to_all | solution.py:54
  88.2 0.6 fusion.8
  88.8 0.7 copy.16
  (49 shorter events, 2.9 us)
Async XLA Ops:
  0.0 39.7 %copy-start = (f32[4,5,32]{2,0,1:T(4,128)S(1)}, f32[4,5,32]{2,0,1:T(4,128)}, u32[]{:S(2)}) copy-start(f32[4,5,32]{2,0,1:T(4,128)} %param.12) | copy-start | bytes 7684
  25.3 14.2 %copy-start.2 = (s32[5]{0:T(128)S(1)}, s32[5]{0:T(128)}, u32[]{:S(2)}) copy-start(s32[5]{0:T(128)} %param.11) | copy-start | bytes 64
  36.3 4.8 %collective-permute-start = (f32[1,8,4608]{2,1,0:T(8,128)}, f32[1,8,4608]{2,1,0:T(8,128)}, u32[]{:S(2)}, u32[]{:S(2)}) collective-permute-start(f32[1,8,4608]{2,1,0:T(8,128)} %get-tuple-element.60), channel_id=1, source_target_pairs={{0,1},{1,0},{2,3},{3,2},{4,5},{5,4},{6,7},{7,6},{8,9},{9,8},{10,11... | collective-permute-start | bytes 442376 | tf_op jit(solution)/shard_map/ppermute | solution.py:20
  36.8 7.5 %collective-permute-start.1 = (f32[1,8,4608]{2,1,0:T(8,128)}, f32[1,8,4608]{2,1,0:T(8,128)}, u32[]{:S(2)}, u32[]{:S(2)}) collective-permute-start(f32[1,8,4608]{2,1,0:T(8,128)} %get-tuple-element.59), channel_id=1, source_target_pairs={{0,2},{1,3},{2,0},{3,1},{4,6},{5,7},{6,4},{7,5},{8,10},{9,11},{10,... | collective-permute-start | bytes 442376 | tf_op jit(solution)/shard_map/ppermute | solution.py:20
  39.3 7.8 %collective-permute-start.2 = (f32[1,8,4608]{2,1,0:T(8,128)}, f32[1,8,4608]{2,1,0:T(8,128)}, u32[]{:S(2)}, u32[]{:S(2)}) collective-permute-start(f32[1,8,4608]{2,1,0:T(8,128)} %get-tuple-element.58), channel_id=1, source_target_pairs={{0,3},{1,2},{2,1},{3,0},{4,7},{5,6},{6,5},{7,4},{8,11},{9,10},{10,... | collective-permute-start | bytes 442376 | tf_op jit(solution)/shard_map/ppermute | solution.py:20
  48.4 10.1 %copy-start.1 = (bf16[2,1,32,4608]{3,2,1,0:T(8,128)(2,1)S(1)}, bf16[2,1,32,4608]{3,2,1,0:T(8,128)(2,1)}, u32[]{:S(2)}) copy-start(bf16[2,1,32,4608]{3,2,1,0:T(8,128)(2,1)} %param.13) | copy-start | bytes 1769476
  52.8 15.8 %all-to-all-start.1 = ((bf16[8,2,9216]{2,1,0:T(2,128)(2,1)}), bf16[8,2,9216]{2,1,0:T(2,128)(2,1)S(1)}, u32[]{:S(2)}, u32[]{:S(2)}) async-start(bf16[8,2,9216]{2,1,0:T(2,128)(2,1)} %reshape.50), calls=%async_computation.1 | async-start | bytes 589824 | tf_op jit(solution)/shard_map/all_to_all | solution.py:71
  68.6 19.6 %all-to-all-start = ((bf16[2,1,32,4608]{3,0,1,2:T(2,128)(2,1)}), bf16[2,1,32,4608]{3,0,1,2:T(2,128)(2,1)S(1)}, u32[]{:S(2)}, u32[]{:S(2)}) async-start(bf16[2,1,32,4608]{3,0,1,2:T(2,128)(2,1)} %copy.14), calls=%async_computation | async-start | bytes 1179648 | tf_op jit(solution)/shard_map/all_to_all | solution.py:54
